TPU v7x, 256 devices: a whole 4x4x8 slice. The times are simulated.
256 devices in a mesh: row: 32 (over y, z), col: 8 (over x, core).
Axes of the slice: x: 4, y: 4, z: 8, core: 2. Of those that a mesh axis runs over, the one named last changes fastest.
Arguments:
- activations: float32 [512, 12288], P('col', 'row'), may hold values from -1.5 to 1.5
- weights: float32 [12288, 24576], P('row', 'col'), may hold values from -0.21875 to 0.21875
- upstream: float32 [512, 24576], P('row', 'col'), may hold values from -6 to 6
Outputs:
- input_grad: float32 [512, 12288], P('col', 'row')
- weight_grad: float32 [12288, 24576], P('row', 'col')
All inputs are finite; a program needn't handle non-finite values.
Results may differ from a plain program's by a relative error of at most 0.00009.
Values sent between devices are 32-bit elements; how exact they have to be, the bound alone decides.
No kernel may reach another device: no remote copies, remote signals or barrier semaphores. Data moves between devices by JAX's collectives and lax.ppermute only.
A program may use at most 64 MiB of HBM per device.

v0:
```python
import jax
import jax.numpy as jnp
from jax import lax
from jax.sharding import Mesh
from jax.sharding import PartitionSpec as P

COL = ("col_0", "col_1")
ROW = ("row_0", "row_1")
slope_scale = 0.7978845608028654
cubic_term = 0.044715


def in_order(blocks, dim):
    blocks = jnp.moveaxis(blocks, 0, dim)
    shape = blocks.shape
    return blocks.reshape(*shape[:dim], shape[dim] * shape[dim + 1], *shape[dim + 2 :])


def all_blocks(x, axes, turns):
    blocks = x[None]
    for k in turns:
        blocks = lax.all_gather(blocks, axes[k], axis=0, tiled=True)
    held = [lax.axis_size(axes[k]) for k in reversed(turns)]
    blocks = blocks.reshape(*held, *x.shape)
    turned = sorted(range(len(turns)), key=lambda place: turns[len(turns) - 1 - place])
    return blocks.transpose(*turned, *range(len(turns), blocks.ndim)).reshape(-1, *x.shape)


def gather_axes(x, axes, turns, dim):
    return in_order(all_blocks(x, axes, turns), dim)


def summed_rows(x, axes, dim):
    for axis in axes:
        x = lax.psum_scatter(x, axis, scatter_dimension=dim, tiled=True)
    return x


def in_blocks(x, dim, length):
    before, after = (x.shape[:dim], x.shape[dim + 1 :])
    return jnp.moveaxis(x.reshape(*before, length, -1, *after), dim, 0)


def summed_on_arrival(x, axis, dim):
    blocks = in_blocks(x, dim, lax.axis_size(axis))
    arrived = lax.all_to_all(blocks, axis, split_axis=0, concat_axis=0, tiled=True)
    return arrived.sum(axis=0)


def gelu_slope(preact):
    inner = slope_scale * (preact + cubic_term * preact * preact * preact)
    tangent = jnp.tanh(inner)
    return 0.5 * (1.0 + tangent) + 0.5 * preact * (1.0 - tangent * tangent) * slope_scale * (
        1.0 + 3.0 * cubic_term * preact * preact
    )


def body(activations, weights, upstream):
    gathered = gather_axes(activations, COL, (0, 1), 0)
    partial_pre = jnp.dot(
        gathered, weights, precision=lax.Precision.HIGHEST, preferred_element_type=jnp.float32
    )
    shares = summed_rows(partial_pre, ROW, 0)
    delta_pre = lax.all_gather(upstream * gelu_slope(shares), ROW, axis=0, tiled=True)
    weight_grad = lax.dot_general(
        gathered,
        delta_pre,
        (((0,), (0,)), ((), ())),
        precision=lax.Precision.HIGHEST,
        preferred_element_type=jnp.float32,
    )
    input_grad = summed_on_arrival(
        lax.dot_general(
            delta_pre,
            weights,
            (((1,), (1,)), ((), ())),
            precision=lax.Precision.HIGHEST,
            preferred_element_type=jnp.float32,
        ),
        COL,
        0,
    )
    return (input_grad, weight_grad)


def solution(mesh):
    torus = Mesh(mesh.devices.reshape(4, 8, 4, 2), ("row_0", "row_1", "col_0", "col_1"))
    in_specs = (P(COL, ROW), P(ROW, COL), P(ROW, COL))
    out_specs = (P(COL, ROW), P(ROW, COL))
    return jax.shard_map(body, mesh=torus, in_specs=in_specs, out_specs=out_specs, check_vma=False)
```

profile of v0, /device:TPU:1, one launch (start us, length us, event | category | flops | bytes accessed | tf_op | source)
XLA Modules:
  0.0 285.1 jit_solution(7580726740365344956)
XLA Ops:
  7.2 0.0 reduce-scatter.3.cloned.1.call-start
  7.2 11.9 %all-gather = f32[256,384]{1,0:T(8,128)S(1)} all-gather(f32[64,384]{1,0:T(8,128)} %param.3), channel_id=2, replica_groups=mesh['row_0'=4,'row_1'=8,'col_0'=4,'col_1'=2] {'col_0'}, dimensions={0}, use_global_device_ids=true | all-gather | bytes 491520 | tf_op jit(solution)/shard_map/all_gather | solution.py:22
  19.1 6.4 %all_gather.10 = f32[8,64,384]{2,1,0:T(8,128)S(1)} all-gather(f32[4,64,384]{2,1,0:T(8,128)S(1)} %bitcast.17), channel_id=1, replica_groups=mesh['row_0'=4,'row_1'=8,'col_0'=4,'col_1'=2] {'col_1'}, dimensions={0}, use_global_device_ids=true | all-gather | bytes 1179648 | tf_op jit(solution)/shard_map/all_gather | solution.py:22
  25.5 0.1 copy.9
  25.6 13.6 %fusion.6 = f32[512,3072]{1,0:T(8,128)} fusion(f32[512,384]{1,0:T(8,128)S(1)} %bitcast.14, f32[384,3072]{1,0:T(8,128)} %param.4), kind=kOutput, calls=%fused_computation.9 | convolution fusion | flops 7247757312 | bytes 11796480 | tf_op jit(solution)/shard_map/dot_general | solution.py:60
  39.2 0.0 copy-start
  39.2 0.0 reduce-scatter.3.cloned.1.call-update
  39.2 0.0 reduce-scatter.5.cloned.1.call-start
  39.3 67.3 %reduce-scatter.3.cloned.1.call-done = f32[128,3072]{1,0:T(8,128)} async-done(((f32[512,3072]{1,0:T(8,128)}), f32[128,3072]{1,0:T(8,128)}) %reduce-scatter.3.cloned.1.call-update) | async-done | bytes 1572880 | tf_op jit(solution)/shard_map/reduce_scatter | solution.py:35
  106.6 0.0 reduce-scatter.5.cloned.1.call-update
  106.6 0.0 all-gather.3.cloned.1.call-start
  106.6 39.0 %reduce-scatter.5.cloned.1.call-done = f32[16,3072]{1,0:T(8,128)} async-done(((f32[128,3072]{1,0:T(8,128)}), f32[16,3072]{1,0:T(8,128)}) %reduce-scatter.5.cloned.1.call-update) | async-done | bytes 196624 | tf_op jit(solution)/shard_map/reduce_scatter | solution.py:35
  145.7 0.0 copy-done
  145.7 1.7 fusion.5
  147.4 0.0 all-gather.3.cloned.1.call-update
  147.4 91.2 %all-gather.3.cloned.1.call-done = f32[512,3072]{1,0:T(8,128)} async-done(((f32[16,3072]{1,0:T(8,128)}), f32[512,3072]{1,0:T(8,128)}) %all-gather.3.cloned.1.call-update) | async-done | bytes 6291472 | tf_op jit(solution)/shard_map/all_gather | solution.py:64
  238.7 13.8 %fusion.7 = f32[512,384]{1,0:T(8,128)} fusion(f32[512,3072]{1,0:T(8,128)} %all-gather.3.cloned.1.call-done, f32[384,3072]{1,0:T(8,128)} %param.4), kind=kOutput, calls=%fused_computation.10 | convolution fusion | flops 7247757312 | bytes 11796480 | tf_op jit(solution)/shard_map/dot_general | solution.py:73
  252.4 5.9 %all-to-all-start = ((f32[8,64,384]{2,1,0:T(8,128)}), f32[8,64,384]{2,1,0:T(8,128)S(1)}, u32[]{:S(2)}, u32[]{:S(2)}) async-start(f32[8,64,384]{2,1,0:T(8,128)} %bitcast.4), calls=%async_computation.2 | async-start | bytes 1572864 | tf_op jit(solution)/shard_map/all_to_all | solution.py:46
  258.3 13.6 %convolution_bitcast_fusion = f32[384,3072]{0,1:T(8,128)} fusion(f32[512,3072]{1,0:T(8,128)} %all-gather.3.cloned.1.call-done, f32[512,384]{1,0:T(8,128)S(1)} %bitcast.15), kind=kOutput, calls=%fused_computation | convolution fusion | flops 7247757312 | bytes 11796480 | tf_op jit(solution)/shard_map/dot_general | solution.py:65
  271.9 6.0 %copy.10 = f32[384,3072]{1,0:T(8,128)} copy(f32[384,3072]{0,1:T(8,128)} %convolution_bitcast_fusion) | data formatting | bytes 9437184
  277.9 0.0 all-to-all-done
  277.9 0.7 reduce_sum.9
Async XLA Ops:
  7.2 99.4 %reduce-scatter.3.cloned.1.call-start = ((), (), s32[]{:S(2)}) async-start(), calls=%async_computation.3 | async-start | bytes 7864320 | tf_op jit(solution)/shard_map/reduce_scatter | solution.py:35
  39.2 106.5 %copy-start = (f32[16,3072]{1,0:T(8,128)S(1)}, f32[16,3072]{1,0:T(8,128)}, u32[]{:S(2)}) copy-start(f32[16,3072]{1,0:T(8,128)} %param.5) | copy-start | bytes 589828
  39.2 106.5 %reduce-scatter.5.cloned.1.call-start = ((), (), s32[]{:S(2)}) async-start(), calls=%async_computation.4 | async-start | bytes 1769472 | tf_op jit(solution)/shard_map/reduce_scatter | solution.py:35
  106.6 132.1 %all-gather.3.cloned.1.call-start = ((), (), s32[]{:S(2)}) async-start(), calls=%async_computation.5 | async-start | bytes 6488064 | tf_op jit(solution)/shard_map/all_gather | solution.py:64
  252.4 25.5 %all-to-all-start = ((f32[8,64,384]{2,1,0:T(8,128)}), f32[8,64,384]{2,1,0:T(8,128)S(1)}, u32[]{:S(2)}, u32[]{:S(2)}) async-start(f32[8,64,384]{2,1,0:T(8,128)} %bitcast.4), calls=%async_computation.2 | async-start | bytes 1572864 | tf_op jit(solution)/shard_map/all_to_all | solution.py:46
Sparse Core Ops, SparseCore 0:
  39.3 67.1 reduce-scatter.2
  109.1 36.5 reduce-scatter.4
  148.8 89.7 all-gather.2
where the time goes:
time: 285 us
  waiting for transfers between devices  198 us (69%)
  matrix products  41 us (14%)
  blocking collectives  18.3 us (6%)
  between operations  13.8 us (5%)
  local copies, waits for them, and re-layouts  6.1 us (2%)
  starting transfers between devices  5.97 us (2%)
    reduce_scatter x2, waiting for transfers between devices, summed_rows(): x = lax.psum_scatter(x, axis, scatter_dimension=dim, tiled=True)  106 us
    all_gather x1, waiting for transfers between devices, body(): lax.all_gather(upstream * gelu_slope(shares), ROW, axis=0, tiled=True)  91.2 us
    all_gather x2, blocking collectives, all_blocks(): blocks = lax.all_gather(blocks, axes[k], axis=0, tiled=True)  18.3 us
    dot_general x1, matrix products, body(): lax.dot_general(delta_pre, weights, (((1,), (1,)), ((), ())), precision=l...  13.8 us
    dot_general x1, matrix products, body(): jnp.dot(gathered, weights, precision=lax.Precision.HIGHEST, preferred_ele...  13.6 us
    dot_general x1, matrix products, body(): lax.dot_general(gathered, delta_pre, (((0,), (0,)), ((), ())), precision=...  13.6 us
    unnamed x3, local copies, waits for them, and re-layouts  6.05 us
    all_to_all x1, starting transfers between devices, summed_on_arrival(): lax.all_to_all(blocks, axis, split_axis=0, concat_axis=0, tiled=True)  5.85 us
  transfers between devices with their start and end apart: 4, of which 3 were waited for; matrix products, arithmetic and copies ran while one was open for 7% of the time, Pallas kernels for 0%

commit v1 on v0

--- a/solution.py
+++ b/solution.py
@@ -61,7 +61,10 @@
         gathered, weights, precision=lax.Precision.HIGHEST, preferred_element_type=jnp.float32
     )
     shares = summed_rows(partial_pre, ROW, 0)
-    delta_pre = lax.all_gather(upstream * gelu_slope(shares), ROW, axis=0, tiled=True)
+    delta_pre = jnp.concatenate(
+        lax.all_to_all(jnp.stack([upstream * gelu_slope(shares)] * lax.axis_size(ROW)), ROW, 0, 0),
+        axis=0,
+    )
     weight_grad = lax.dot_general(
         gathered,
         delta_pre,

time: 285 us -> 342 us (1.20)
  blocking collectives: 18.3 us -> 158 us
  waiting for transfers between devices: 198 us -> 106 us
  starting transfers between devices: 5.97 us -> 13.5 us
    all_to_all x0 -> x1, blocking collectives: none -> 140 us  [body(): lax.all_to_all(jnp.stack([upstream * gelu_slope(shares)] * lax.axis_size(...]
    all_gather x1 -> x0, waiting for transfers between devices: 91.2 us -> none  [body(): lax.all_gather(upstream * gelu_slope(shares), ROW, axis=0, tiled=True)]
    all_to_all x1, starting transfers between devices: 5.85 us -> 13.4 us  [summed_on_arrival(): lax.all_to_all(blocks, axis, split_axis=0, concat_axis=0, tiled=True)]
    unnamed x3 -> x9, local copies, waits for them, and re-layouts: 6.05 us -> 8.71 us
  transfers between devices with their start and end apart: 4 -> 3, of which waited for: 3 -> 2; matrix products, arithmetic and copies ran while one was open for 7% -> 6% of each run, Pallas kernels for 0% -> 0%
where the time goes in v1:
time: 342 us
  blocking collectives  158 us (46%)
  waiting for transfers between devices  106 us (31%)
  matrix products  38.2 us (11%)
  between operations  14.1 us (4%)
  starting transfers between devices  13.5 us (4%)
  local copies, waits for them, and re-layouts  9.51 us (3%)
    all_to_all x1, blocking collectives, body(): lax.all_to_all(jnp.stack([upstream * gelu_slope(shares)] * lax.axis_size(...  140 us
    reduce_scatter x2, waiting for transfers between devices, summed_rows(): x = lax.psum_scatter(x, axis, scatter_dimension=dim, tiled=True)  106 us
    all_gather x2, blocking collectives, all_blocks(): blocks = lax.all_gather(blocks, axes[k], axis=0, tiled=True)  18.3 us
    dot_general x1, matrix products, body(): jnp.dot(gathered, weights, precision=lax.Precision.HIGHEST, preferred_ele...  13.6 us
    dot_general x1, matrix products, body(): lax.dot_general(gathered, delta_pre, (((0,), (0,)), ((), ())), precision=...  13.6 us
    all_to_all x1, starting transfers between devices, summed_on_arrival(): lax.all_to_all(blocks, axis, split_axis=0, concat_axis=0, tiled=True)  13.4 us
    dot_general x1, matrix products, body(): lax.dot_general(delta_pre, weights, (((1,), (1,)), ((), ())), precision=l...  11 us
    unnamed x9, local copies, waits for them, and re-layouts  8.71 us
  transfers between devices with their start and end apart: 3, of which 2 were waited for; matrix products, arithmetic and copies ran while one was open for 6% of the time, Pallas kernels for 0%

profile of v1, /device:TPU:1, one launch (start us, length us, event | category | flops | bytes accessed | tf_op | source)
XLA Modules:
  0.0 341.9 jit_solution(10398972300342429925)
XLA Ops:
  7.2 0.0 reduce-scatter.3.cloned.1.call-start
  7.2 11.9 %all-gather = f32[256,384]{1,0:T(8,128)S(1)} all-gather(f32[64,384]{1,0:T(8,128)} %param.3), channel_id=2, replica_groups=mesh['row_0'=4,'row_1'=8,'col_0'=4,'col_1'=2] {'col_0'}, dimensions={0}, use_global_device_ids=true | all-gather | bytes 491520 | tf_op jit(solution)/shard_map/all_gather | solution.py:22
  19.1 6.4 %all_gather.7 = f32[8,64,384]{2,1,0:T(8,128)S(1)} all-gather(f32[4,64,384]{2,1,0:T(8,128)S(1)} %bitcast.24), channel_id=1, replica_groups=mesh['row_0'=4,'row_1'=8,'col_0'=4,'col_1'=2] {'col_1'}, dimensions={0}, use_global_device_ids=true | all-gather | bytes 1179648 | tf_op jit(solution)/shard_map/all_gather | solution.py:22
  25.5 0.1 copy.9
  25.6 13.6 %fusion.8 = f32[512,3072]{1,0:T(8,128)} fusion(f32[512,384]{1,0:T(8,128)S(1)} %bitcast.21, f32[384,3072]{1,0:T(8,128)} %param.4), kind=kOutput, calls=%fused_computation.11 | convolution fusion | flops 7247757312 | bytes 11796480 | tf_op jit(solution)/shard_map/dot_general | solution.py:60
  39.2 0.0 copy-start.1
  39.2 0.0 reduce-scatter.3.cloned.1.call-update
  39.2 0.0 reduce-scatter.5.cloned.1.call-start
  39.3 67.3 %reduce-scatter.3.cloned.1.call-done = f32[128,3072]{1,0:T(8,128)} async-done(((f32[512,3072]{1,0:T(8,128)}), f32[128,3072]{1,0:T(8,128)}) %reduce-scatter.3.cloned.1.call-update) | async-done | bytes 1572880 | tf_op jit(solution)/shard_map/reduce_scatter | solution.py:35
  106.6 0.0 reduce-scatter.5.cloned.1.call-update
  106.6 39.1 %reduce-scatter.5.cloned.1.call-done = f32[16,3072]{1,0:T(8,128)} async-done(((f32[128,3072]{1,0:T(8,128)}), f32[16,3072]{1,0:T(8,128)}) %reduce-scatter.5.cloned.1.call-update) | async-done | bytes 196624 | tf_op jit(solution)/shard_map/reduce_scatter | solution.py:35
  145.7 0.0 copy-done.1
  145.7 1.1 fusion.7
  146.8 0.0 slice-start
  146.8 0.8 stack.2
  147.5 0.0 slice-start.1
  147.5 140.1 %all_to_all.10 = f32[32,16,3072]{2,1,0:T(8,128)S(1)} all-to-all(f32[32,16,3072]{2,1,0:T(8,128)S(1)} %stack.2), channel_id=1, replica_groups=mesh['row_0'=4,'row_1'=8,'col_0'=4,'col_1'=2] {'row_0','row_1'}, dimensions={0} | all-to-all | bytes 12582912 | tf_op jit(solution)/shard_map/all_to_all | solution.py:65
  287.7 0.0 copy-start
  287.7 2.6 copy-done
  290.3 0.0 slice-done
  290.3 0.0 slice-done.1
  290.3 11.0 %fusion = f32[8,64,384]{2,1,0:T(8,128)} fusion(f32[8,64,3072]{2,1,0:T(8,128)S(1)} %bitcast.17, f32[384,3072]{1,0:T(8,128)S(1)} %bitcast.20), kind=kOutput, calls=%fused_computation | convolution fusion | flops 7247757312 | bytes 11796480 | tf_op jit(solution)/shard_map/dot_general | solution.py:76
  301.3 13.4 %all-to-all-start.1 = ((f32[8,64,384]{2,1,0:T(8,128)}), f32[8,64,384]{2,1,0:T(8,128)S(1)}, u32[]{:S(2)}, u32[]{:S(2)}) async-start(f32[8,64,384]{2,1,0:T(8,128)} %fusion), calls=%async_computation.3 | async-start | bytes 1572864 | tf_op jit(solution)/shard_map/all_to_all | solution.py:46
  314.7 13.6 %convolution_bitcast_fusion = f32[384,3072]{0,1:T(8,128)} fusion(f32[512,3072]{1,0:T(8,128)} %bitcast.18, f32[512,384]{1,0:T(8,128)S(1)} %bitcast.22), kind=kOutput, calls=%fused_computation.2 | convolution fusion | flops 7247757312 | bytes 11796480 | tf_op jit(solution)/shard_map/dot_general | solution.py:68
  328.3 6.0 %copy.10 = f32[384,3072]{1,0:T(8,128)} copy(f32[384,3072]{0,1:T(8,128)} %convolution_bitcast_fusion) | data formatting | bytes 9437184
  334.3 0.0 all-to-all-done.1
  334.3 0.7 reduce_sum.9
  (1 shorter events, 0.0 us)
Async XLA Ops:
  7.2 99.4 %reduce-scatter.3.cloned.1.call-start = ((), (), s32[]{:S(2)}) async-start(), calls=%async_computation.4 | async-start | bytes 7864320 | tf_op jit(solution)/shard_map/reduce_scatter | solution.py:35
  39.2 106.5 %copy-start.1 = (f32[16,3072]{1,0:T(8,128)S(1)}, f32[16,3072]{1,0:T(8,128)}, u32[]{:S(2)}) copy-start(f32[16,3072]{1,0:T(8,128)} %param.5) | copy-start | bytes 589828
  39.2 106.5 %reduce-scatter.5.cloned.1.call-start = ((), (), s32[]{:S(2)}) async-start(), calls=%async_computation.5 | async-start | bytes 1769472 | tf_op jit(solution)/shard_map/reduce_scatter | solution.py:35
  146.8 143.6 %slice-start = ((s8[4718592]{0:T(1024)(128)(4,1)}), s8[4194304]{0:T(1024)(128)(4,1)S(1)}, s32[]{:S(2)}) async-start(s8[4718592]{0:T(1024)(128)(4,1)} %bitcast.19), calls=%async_computation.6 | async-start | bytes 8388608
  147.5 142.8 %slice-start.1 = ((s8[4718592]{0:T(1024)(128)(4,1)}), s8[524288]{0:T(1024)(128)(4,1)S(1)}, s32[]{:S(2)}) async-start(s8[4718592]{0:T(1024)(128)(4,1)} %bitcast.19), calls=%async_computation.7 | async-start | bytes 1048576
  287.7 2.6 copy-start
  301.3 33.0 %all-to-all-start.1 = ((f32[8,64,384]{2,1,0:T(8,128)}), f32[8,64,384]{2,1,0:T(8,128)S(1)}, u32[]{:S(2)}, u32[]{:S(2)}) async-start(f32[8,64,384]{2,1,0:T(8,128)} %fusion), calls=%async_computation.3 | async-start | bytes 1572864 | tf_op jit(solution)/shard_map/all_to_all | solution.py:46
Sparse Core Ops, SparseCore 0:
  39.3 67.1 reduce-scatter.2
  109.1 36.5 reduce-scatter.4
